TPU v7x, 32 devices: a whole 2x2x4 slice. The times are simulated.
32 devices in a mesh: dp: 2 (over x), expert: 16 (over z, y, core).
Axes of the slice: x: 2, y: 2, z: 4, core: 2. Of those that a mesh axis runs over, the one named last changes fastest.
Arguments:
- tokens: bfloat16 [4096, 1024], P(('dp', 'expert')), may hold values from -6 to 6
- out_grad: bfloat16 [4096, 1024], P(('dp', 'expert')), may hold values from -6 to 6
- expert_ids: int32 [4096, 3], P(('dp', 'expert')), may hold values from 0 to 15, all different within a row; in each aligned block of 128 rows (0 to 127, 128 to 255, ...) at most 30 rows name the same one
- gate_probs: float32 [4096, 3], P(('dp', 'expert')), may hold values from 0.1 to 0.6
- saved_pre: bfloat16 [2, 16, 480, 1536], P('dp', 'expert'), may hold values from -6 to 6
- gate_weight: bfloat16 [16, 1024, 768], P('expert', 'dp'), may hold values from -0.1875 to 0.1875
- up_weight: bfloat16 [16, 1024, 768], P('expert', 'dp'), may hold values from -0.1875 to 0.1875
- down_weight: bfloat16 [16, 1024, 768], P('expert', 'dp'), may hold values from -0.21875 to 0.21875
- basis: bfloat16 [16, 1024, 256], P('expert', 'dp'), may hold values from -0.1875 to 0.1875
Outputs:
- in_grad: bfloat16 [4096, 1024], P(('dp', 'expert'))
- proj_grads: float32 [16, 3, 256, 768], P('expert', None, 'dp')
Inputs may be any that keep to these rules, and one draw needn't show every extreme that they name: `expert_ids`: each token names 3 different experts. The rows of one device name one expert at most 30 times, and on some devices some expert exactly 30 times.
All inputs are finite; a program needn't handle non-finite values.
Results may differ from a plain program's by a relative error of at most 0.0091.
Values may be sent and summed in bfloat16 or wider, within the bound.
A program may use at most 64 MiB of HBM per device.

v0:
```python
import jax
import jax.numpy as jnp
from jax import lax
from jax.sharding import PartitionSpec as P


def contract_rows(left, right):
    return lax.dot_general(
        left, right, (((0,), (0,)), ((), ())), preferred_element_type=jnp.float32
    )


def contract_cols(left, right):
    return lax.dot_general(
        left, right, (((1,), (1,)), ((), ())), preferred_element_type=jnp.float32
    )


def body(
    tokens, out_grad, expert_ids, gate_probs, saved_pre, gate_weight, up_weight, down_weight, basis
):
    n_owner = lax.axis_size("expert")
    tok_rows, width = tokens.shape
    topk = expert_ids.shape[1]
    slots = saved_pre.shape[2]
    cap = slots // n_owner
    hidden = gate_weight.shape[2]
    onehot = (expert_ids[:, :, None] == jnp.arange(n_owner, dtype=jnp.int32)[None, None, :]).astype(
        jnp.int32
    )
    per_token = jnp.sum(onehot, axis=1)
    before = jnp.cumsum(per_token, axis=0) - per_token
    position = jnp.sum(onehot * before[:, None, :], axis=2)
    target = expert_ids * cap + position
    token_index = jnp.broadcast_to(jnp.arange(tok_rows, dtype=jnp.int32)[:, None], target.shape)
    choice_index = jnp.broadcast_to(jnp.arange(topk, dtype=jnp.int32)[None, :], target.shape)
    fill_token = (
        jnp.full((n_owner * cap,), -1, jnp.int32)
        .at[target.reshape(-1)]
        .set(token_index.reshape(-1))
    )
    fill_choice = (
        jnp.zeros((n_owner * cap,), jnp.int32).at[target.reshape(-1)].set(choice_index.reshape(-1))
    )
    filled = fill_token >= 0
    picked = jnp.maximum(fill_token, 0)
    send_rows = jnp.where(filled[:, None], tokens[picked], jnp.zeros((), jnp.bfloat16))
    weight_pick = gate_probs[picked, fill_choice]
    scaled = (out_grad[picked].astype(jnp.float32) * weight_pick[:, None]).astype(jnp.bfloat16)
    send_grad = jnp.where(filled[:, None], scaled, jnp.zeros((), jnp.bfloat16))
    arrived_rows, arrived_grad = (
        lax.all_to_all(
            send_rows.reshape(n_owner, cap, width),
            "expert",
            split_axis=0,
            concat_axis=0,
            tiled=True,
        ),
        lax.all_to_all(
            send_grad.reshape(n_owner, cap, width),
            "expert",
            split_axis=0,
            concat_axis=0,
            tiled=True,
        ),
    )
    rows_in = arrived_rows.reshape(slots, width)
    grad_in = arrived_grad.reshape(slots, width)
    pieces = (
        lax.all_gather(down_weight, "dp", axis=1, tiled=True),
        lax.all_gather(basis, "dp", axis=1, tiled=True),
    )
    down_piece = pieces[0][0]
    basis_piece = pieces[1][0]
    hidden_grad = jnp.dot(grad_in, down_piece, preferred_element_type=jnp.float32)
    x_acc = jnp.dot(rows_in, basis_piece, preferred_element_type=jnp.float32)
    dy_acc = jnp.dot(grad_in, basis_piece, preferred_element_type=jnp.float32)
    hidden_grad, x_acc, dy_acc = (hidden_grad, x_acc, dy_acc)
    pre = saved_pre[0, 0].astype(jnp.float32)
    gate_pre = pre[:, :hidden]
    up_pre = pre[:, hidden:]
    sig = jax.nn.sigmoid(gate_pre)
    hid = (gate_pre * sig * up_pre).astype(jnp.bfloat16)
    up_grad = (hidden_grad * gate_pre * sig).astype(jnp.bfloat16)
    gate_grad = (hidden_grad * up_pre * sig * (1.0 + gate_pre * (1.0 - sig))).astype(jnp.bfloat16)
    x_proj = x_acc.astype(jnp.bfloat16)
    dy_proj = dy_acc.astype(jnp.bfloat16)
    pieces = lax.all_gather((gate_weight, up_weight), "dp", axis=1, tiled=True)
    row_grad = contract_cols(gate_grad, pieces[0][0]) + contract_cols(up_grad, pieces[1][0])
    terms = jnp.stack(
        [
            contract_rows(x_proj, gate_grad),
            contract_rows(x_proj, up_grad),
            contract_rows(dy_proj, hid),
        ]
    )
    proj_grads = lax.psum_scatter(terms[None], "dp", scatter_dimension=2, tiled=True)
    returned = lax.all_to_all(
        row_grad.astype(jnp.bfloat16).reshape(n_owner, cap, width),
        "expert",
        split_axis=0,
        concat_axis=0,
        tiled=True,
    )
    returned = returned.reshape(n_owner * cap, width)
    in_grad = jnp.sum(returned[target].astype(jnp.float32), axis=1).astype(jnp.bfloat16)
    return (in_grad, proj_grads)


def solution(mesh):
    return jax.shard_map(
        body,
        mesh=mesh,
        in_specs=(
            P(("dp", "expert"), None),
            P(("dp", "expert"), None),
            P(("dp", "expert"), None),
            P(("dp", "expert"), None),
            P("dp", "expert", None, None),
            P("expert", "dp", None),
            P("expert", "dp", None),
            P("expert", "dp", None),
            P("expert", "dp", None),
        ),
        out_specs=(P(("dp", "expert"), None), P("expert", None, "dp", None)),
        check_vma=False,
    )
```

profile of v0, /device:TPU:0, one launch (start us, length us, event | category | flops | bytes accessed | tf_op | source)
XLA Modules:
  0.0 153.1 jit_solution(18222967836924440757)
XLA Ops:
  7.2 0.7 all-gather.4.cloned.1.call-update
  7.9 0.7 convert_reduce_fusion
  8.6 0.1 copy.15
  8.7 0.2 reduce_window_sum.11
  8.9 0.7 select_reduce_fusion
  9.7 0.7 compare_select_fusion.1
  10.4 0.1 copy.18
  10.5 0.2 reshape.88
  10.7 0.2 reshape.131
  10.9 0.2 reshape.139
  11.1 2.9 %scatter_custom_fusion.1 = s32[480]{0:T(512)S(1)} fusion(s32[384]{0:T(512)S(1)} %fusion.12, s32[384]{0:T(512)S(1)} %reshape.139, s32[]{:T(128)} %constant.9.clone.1), kind=kCustom, calls=%fused_computation.41 | custom fusion | bytes 1924 | tf_op jit(solution)/shard_map/scatter | solution.py:43
  14.1 2.9 %scatter_custom_fusion = s32[480]{0:T(512)S(1)} fusion(s32[384]{0:T(512)S(1)} %fusion.12, s32[384]{0:T(512)S(1)} %reshape.131, s32[]{:T(128)} %constant.7.clone.1), kind=kCustom, calls=%fused_computation.45 | custom fusion | bytes 1924 | tf_op jit(solution)/shard_map/scatter | solution.py:40
  17.0 2.8 %gather_fusion = bf16[480,1024]{1,0:T(8,128)(2,1)} fusion(bf16[128,1024]{1,0:T(8,128)(2,1)S(1)} %copy-done, s32[1024]{0:T(1024)S(1)} %pad_clamp_fusion.1), kind=kCustom, calls=%fused_computation | custom fusion | bytes 1968000 | tf_op jit(solution)/shard_map/gather | solution.py:49
  19.8 1.4 reshape.95
  21.3 2.8 %gather_fusion.3 = bf16[480,1024]{1,0:T(8,128)(2,1)} fusion(bf16[128,1024]{1,0:T(8,128)(2,1)S(1)} %copy-done.2, s32[1024]{0:T(1024)S(1)} %pad_clamp_fusion.1), kind=kCustom, calls=%fused_computation.3 | custom fusion | bytes 1968000 | tf_op jit(solution)/shard_map/gather | solution.py:47
  24.0 1.4 gather.18
  25.5 4.6 %gather_fusion.1 = f32[480]{0:T(512)S(1)} fusion(f32[128,3]{0,1:T(4,128)S(1)} %copy-done.1, s32[480]{0:T(512)S(1)} %get-tuple-element.8), kind=kCustom, calls=%fused_computation.1 | custom fusion | bytes 7680 | tf_op jit(solution)/shard_map/gather | solution.py:48
  30.2 0.1 broadcast_in_dim.57
  30.3 1.7 %broadcast_select_fusion = (bf16[16,30,1024]{2,1,0:T(8,128)(2,1)}, bf16[16,30,1024]{2,1,0:T(8,128)(2,1)}) fusion(bf16[16,30,1024]{2,1,0:T(8,128)(2,1)S(1)} %gather.18, pred[16,30]{1,0:T(8,128)(4,1)S(1)} %broadcast_in_dim.57, f32[16,30,1024]{2,1,0:T(8,128)S(1)} %reshape.95, f32[16,30]{1,0:T(8,128)S(1)} %mul.53), kind=kLoop, calls=%fused_computation.25 | loop fusion | flops 1966080 | bytes 4917600 | tf_op jit(solution)/shard_map/jit(_where)/select_n | solution.py:47
  32.0 7.4 %all-to-all-start.2 = ((bf16[16,30,1024]{2,1,0:T(8,128)(2,1)}), bf16[16,30,1024]{2,1,0:T(8,128)(2,1)S(1)}, u32[]{:S(2)}, u32[]{:S(2)}) async-start(bf16[16,30,1024]{2,1,0:T(8,128)(2,1)} %get-tuple-element.6), calls=%async_computation.2 | async-start | bytes 2097152 | tf_op jit(solution)/shard_map/all_to_all | solution.py:52
  39.5 0.7 all-gather.6.cloned.1.call-update
  40.2 22.1 %all-to-all-done.2 = bf16[16,30,1024]{2,1,0:T(8,128)(2,1)S(1)} async-done(((bf16[16,30,1024]{2,1,0:T(8,128)(2,1)}), bf16[16,30,1024]{2,1,0:T(8,128)(2,1)S(1)}, u32[]{:S(2)}, u32[]{:S(2)}) %all-to-all-start.2) | async-done | bytes 983072 | tf_op jit(solution)/shard_map/all_to_all | solution.py:52
  62.3 6.8 %all-to-all-start = ((bf16[16,30,1024]{2,1,0:T(8,128)(2,1)}), bf16[16,30,1024]{2,1,0:T(8,128)(2,1)S(1)}, u32[]{:S(2)}, u32[]{:S(2)}) async-start(bf16[16,30,1024]{2,1,0:T(8,128)(2,1)} %get-tuple-element.7), calls=%async_computation | async-start | bytes 2097152 | tf_op jit(solution)/shard_map/all_to_all | solution.py:59
  69.1 0.7 all-gather.8.cloned.1.call-update
  69.9 9.5 %all_gather.15 = bf16[1,1024,256]{2,1,0:T(8,128)(2,1)S(1)} all-gather(bf16[1,512,256]{2,1,0:T(8,128)(2,1)S(1)} %copy-done.7), channel_id=1, replica_groups=mesh['dp'=2,'expert'=16] {'dp'}, dimensions={1}, use_global_device_ids=true | all-gather | bytes 786432 | tf_op jit(solution)/shard_map/all_gather | solution.py:71
  79.4 3.7 %bitcast_convert_fusion = f32[480,1536]{1,0:T(8,128)} fusion(bf16[1,1,480,1536]{3,2,1,0:T(8,128)(2,1)} %param.13), kind=kLoop, calls=%fused_computation.14 | loop fusion | flops 737280 | bytes 4423680 | tf_op jit(solution)/shard_map/convert_element_type | solution.py:79
  83.0 1.2 reshape.94
  84.2 1.6 %convolution_convert_fusion.1 = bf16[480,256]{1,0:T(8,128)(2,1)S(1)} fusion(bf16[480,1024]{1,0:T(8,128)(2,1)} %reshape.94, bf16[1,1024,256]{2,1,0:T(8,128)(2,1)S(1)} %all_gather.15), kind=kOutput, calls=%fused_computation.23 | convolution fusion | flops 251781120 | bytes 1753088 | tf_op jit(solution)/shard_map/dot_general | solution.py:76
  85.8 6.1 %all-to-all-done = bf16[16,30,1024]{2,1,0:T(8,128)(2,1)S(1)} async-done(((bf16[16,30,1024]{2,1,0:T(8,128)(2,1)}), bf16[16,30,1024]{2,1,0:T(8,128)(2,1)S(1)}, u32[]{:S(2)}, u32[]{:S(2)}) %all-to-all-start) | async-done | bytes 983072 | tf_op jit(solution)/shard_map/all_to_all | solution.py:59
  92.0 0.3 reshape.91
  92.3 3.8 %multiply_convert_fusion.2 = (bf16[480,768]{1,0:T(8,128)(2,1)S(1)}, bf16[480,768]{1,0:T(8,128)(2,1)S(1)}) fusion(f32[480,1536]{1,0:T(8,128)} %bitcast_convert_fusion, bf16[480,1024]{1,0:T(8,128)(2,1)S(1)} %reshape.91, bf16[1,1024,768]{2,1,0:T(8,128)(2,1)} %all-gather.4.cloned.1.call-done), kind=kOutput, calls=%fused_computation.16 | convolution fusion | flops 759767040 | bytes 6979584 | tf_op jit(solution)/shard_map/dot_general | solution.py:75
  96.1 0.4 convolution_bitcast_fusion.2
  96.5 0.5 copy-done.4
  97.0 0.4 convolution_bitcast_fusion.1
  97.4 3.4 %convolution_bitcast_fusion = f32[1,256,768]{2,1,0:T(8,128)S(1)} fusion(bf16[480,1024]{1,0:T(8,128)(2,1)} %copy-done.3, f32[480,1536]{1,0:T(8,128)} %bitcast_convert_fusion, bf16[1,1024,256]{2,1,0:T(8,128)(2,1)} %copy-done.6), kind=kOutput, calls=%fused_computation.19 | convolution fusion | flops 442736640 | bytes 5242880 | tf_op jit(solution)/shard_map/dot_general | solution.py:8
  100.8 1.6 %maximum_bitcast_fusion = f32[1,3,256,768]{3,2,1,0:T(8,128)} fusion(f32[1,256,768]{2,1,0:T(8,128)S(1)} %convolution_bitcast_fusion, f32[1,256,768]{2,1,0:T(8,128)S(1)} %convolution_bitcast_fusion.1, f32[1,256,768]{2,1,0:T(8,128)S(1)} %convolution_bitcast_fusion.2), kind=kLoop, calls=%fused_computation.6 | loop fusion | flops 1179648 | bytes 4718592 | tf_op jit(solution)/shard_map/broadcast_in_dim | solution.py:97
  102.5 1.1 copy-done.5
  103.6 3.7 %fusion.1 = f32[480,1024]{1,0:T(8,128)} fusion(bf16[480,768]{1,0:T(8,128)(2,1)S(1)} %copy-done.5, bf16[1,1024,768]{2,1,0:T(8,128)(2,1)} %all-gather.6.cloned.1.call-done), kind=kOutput, calls=%fused_computation.10 | convolution fusion | flops 754974720 | bytes 4276224 | tf_op jit(solution)/shard_map/dot_general | solution.py:14
  107.3 3.0 %add_convert_fusion = bf16[480,1024]{1,0:T(8,128)(2,1)S(1)} fusion(f32[480,1024]{1,0:T(8,128)} %fusion.1, bf16[480,768]{1,0:T(8,128)(2,1)S(1)} %get-tuple-element.4, bf16[1,1024,768]{2,1,0:T(8,128)(2,1)} %all-gather.8.cloned.1.call-done), kind=kOutput, calls=%fused_computation.8 | convolution fusion | flops 755957760 | bytes 5259264 | tf_op jit(solution)/shard_map/dot_general | solution.py:14
  110.2 1.2 reshape.92
  111.5 7.2 %all-to-all-start.1 = ((bf16[16,30,1024]{2,1,0:T(8,128)(2,1)}), bf16[16,30,1024]{2,1,0:T(8,128)(2,1)S(1)}, u32[]{:S(2)}, u32[]{:S(2)}) async-start(bf16[16,30,1024]{2,1,0:T(8,128)(2,1)} %reshape.92), calls=%async_computation.1 | async-start | bytes 2097152 | tf_op jit(solution)/shard_map/all_to_all | solution.py:98
  118.7 0.1 copy.19
  118.8 0.2 reshape.113
  119.0 22.6 %all-to-all-done.1 = bf16[16,30,1024]{2,1,0:T(8,128)(2,1)S(1)} async-done(((bf16[16,30,1024]{2,1,0:T(8,128)(2,1)}), bf16[16,30,1024]{2,1,0:T(8,128)(2,1)S(1)}, u32[]{:S(2)}, u32[]{:S(2)}) %all-to-all-start.1) | async-done | bytes 983072 | tf_op jit(solution)/shard_map/all_to_all | solution.py:98
  141.6 0.3 reshape.93
  141.8 2.1 %gather_fusion.2 = bf16[384,1024]{1,0:T(8,128)(2,1)S(1)} fusion(bf16[480,1024]{1,0:T(8,128)(2,1)S(1)} %reshape.93, s32[1024]{0:T(1024)S(1)} %pad_clamp_fusion), kind=kCustom, calls=%fused_computation.2 | custom fusion | bytes 1574400 | tf_op jit(solution)/shard_map/gather | solution.py:106
  143.9 0.5 reshape.116
  144.4 2.1 %reduce_sum.32 = bf16[128,1024]{1,0:T(8,128)(2,1)} reduce(bf16[128,3,1024]{2,1,0:T(4,128)(2,1)S(1)} %reshape.116, bf16[]{:T(256)} %constant.12.clone.1), dimensions={1}, to_apply=%region_5.6 | reduce | flops 262144 | bytes 1048578 | tf_op jit(solution)/shard_map/reduce_sum | solution.py:106
  (33 shorter events, 0.5 us)
Async XLA Ops:
  7.2 9.9 %copy-start = (bf16[128,1024]{1,0:T(8,128)(2,1)S(1)}, bf16[128,1024]{1,0:T(8,128)(2,1)}, u32[]{:S(2)}) copy-start(bf16[128,1024]{1,0:T(8,128)(2,1)} %param.10) | copy-start | bytes 786436
  7.2 85.1 %all-gather.4.cloned.1.call-start = ((), (), s32[]{:S(2)}) async-start(), calls=%async_computation.4 | async-start | bytes 2359296 | tf_op jit(solution)/shard_map/all_gather | solution.py:70
  19.8 1.5 copy-start.2
  24.0 1.5 copy-start.1
  32.0 30.3 %all-to-all-start.2 = ((bf16[16,30,1024]{2,1,0:T(8,128)(2,1)}), bf16[16,30,1024]{2,1,0:T(8,128)(2,1)S(1)}, u32[]{:S(2)}, u32[]{:S(2)}) async-start(bf16[16,30,1024]{2,1,0:T(8,128)(2,1)} %get-tuple-element.6), calls=%async_computation.2 | async-start | bytes 2097152 | tf_op jit(solution)/shard_map/all_to_all | solution.py:52
  39.4 63.1 %all-gather.6.cloned.1.call-start = ((), (), s32[]{:S(2)}) async-start(), calls=%async_computation.5 | async-start | bytes 2359296 | tf_op jit(solution)/shard_map/all_gather | solution.py:88
  40.2 29.7 %copy-start.7 = (bf16[1,512,256]{2,1,0:T(8,128)(2,1)S(1)}, bf16[1,512,256]{2,1,0:T(8,128)(2,1)}, u32[]{:S(2)}) copy-start(bf16[1,512,256]{2,1,0:T(8,128)(2,1)} %param.17) | copy-start | bytes 786436
  62.3 29.7 %all-to-all-start = ((bf16[16,30,1024]{2,1,0:T(8,128)(2,1)}), bf16[16,30,1024]{2,1,0:T(8,128)(2,1)S(1)}, u32[]{:S(2)}, u32[]{:S(2)}) async-start(bf16[16,30,1024]{2,1,0:T(8,128)(2,1)} %get-tuple-element.7), calls=%async_computation | async-start | bytes 2097152 | tf_op jit(solution)/shard_map/all_to_all | solution.py:59
  69.1 38.2 %all-gather.8.cloned.1.call-start = ((), (), s32[]{:S(2)}) async-start(), calls=%async_computation.6 | async-start | bytes 2359296 | tf_op jit(solution)/shard_map/all_gather | solution.py:88
  69.8 76.7 %reduce-scatter.2.cloned.1.call-start = ((), (), s32[]{:S(2)}) async-start(), calls=%async_computation.7 | async-start | bytes 3538944 | tf_op jit(solution)/shard_map/reduce_scatter | solution.py:97
  79.3 4.9 %copy-start.6 = (bf16[1,1024,256]{2,1,0:T(8,128)(2,1)}, bf16[1,1024,256]{2,1,0:T(8,128)(2,1)S(1)}, u32[]{:S(2)}) copy-start(bf16[1,1024,256]{2,1,0:T(8,128)(2,1)S(1)} %all_gather.15) | copy-start | bytes 1572868
  92.2 3.9 %copy-start.3 = (bf16[480,1024]{1,0:T(8,128)(2,1)}, bf16[480,1024]{1,0:T(8,128)(2,1)S(1)}, u32[]{:S(2)}) copy-start(bf16[480,1024]{1,0:T(8,128)(2,1)S(1)} %reshape.91) | copy-start | bytes 2949124
  96.1 0.9 copy-start.4
  102.5 1.1 copy-start.5
  111.5 30.1 %all-to-all-start.1 = ((bf16[16,30,1024]{2,1,0:T(8,128)(2,1)}), bf16[16,30,1024]{2,1,0:T(8,128)(2,1)S(1)}, u32[]{:S(2)}, u32[]{:S(2)}) async-start(bf16[16,30,1024]{2,1,0:T(8,128)(2,1)} %reshape.92), calls=%async_computation.1 | async-start | bytes 2097152 | tf_op jit(solution)/shard_map/all_to_all | solution.py:98
Sparse Core Ops, SparseCore 0:
  9.5 29.8 all-gather.3
  41.8 28.4 all-gather.5
  71.8 28.0 all-gather.7
  102.6 36.8 reduce-scatter.1
where the time goes:
time: 155 us; the launch traced here: 153 us
  waiting for transfers between devices  52.9 us (34%)
  local copies, waits for them, and re-layouts  27.4 us (18%)
  starting transfers between devices  21.5 us (14%)
  matrix products  16.3 us (11%)
  between operations  14 us (9%)
  other arithmetic  11.4 us (7%)
  blocking collectives  9.46 us (6%)
    all_to_all x1, waiting for transfers between devices, body(): lax.all_to_all(row_grad.astype(jnp.bfloat16).reshape(n_owner, cap, width)...  22.6 us
    all_to_all x1, waiting for transfers between devices, body(): lax.all_to_all(send_rows.reshape(n_owner, cap, width), 'expert', split_ax...  22.1 us
    all_gather x1, blocking collectives, body(): lax.all_gather(basis, 'dp', axis=1, tiled=True)  9.46 us
    all_to_all x1, starting transfers between devices, body(): lax.all_to_all(send_rows.reshape(n_owner, cap, width), 'expert', split_ax...  7.4 us
    all_to_all x1, starting transfers between devices, body(): lax.all_to_all(row_grad.astype(jnp.bfloat16).reshape(n_owner, cap, width)...  7.2 us
    all_to_all x1, starting transfers between devices, body(): lax.all_to_all(send_grad.reshape(n_owner, cap, width), 'expert', split_ax...  6.79 us
    dot_general x2, matrix products, contract_cols(): lax.dot_general(left, right, (((1,), (1,)), ((), ())), preferred_element_...  6.64 us
    all_to_all x1, waiting for transfers between devices, body(): lax.all_to_all(send_grad.reshape(n_owner, cap, width), 'expert', split_ax...  6.14 us
  transfers between devices with their start and end apart: 7, of which 3 were waited for; matrix products, arithmetic and copies ran while one was open for 35% of the time, Pallas kernels for 0%

commit v1 on v0

v1 whole, which is shorter than its diff:
```python
import functools
import jax
import jax.numpy as jnp
from jax import lax
from jax.experimental import pallas as pl
from jax.experimental.pallas import tpu as pltpu
from jax.sharding import PartitionSpec as P

MESH = pl.DeviceIdType.MESH
F32 = jnp.float32
BF16 = jnp.bfloat16


def dot(left, right, dims):
    return lax.dot_general(left, right, (dims, ((), ())), preferred_element_type=F32)


NN = ((1,), (0,))
TN = ((0,), (0,))
NT = ((1,), (1,))


def kernel(
    n_dp, n_ex, cap, cp, cw,
    ids, probs, tok, og, pre_h, gw, uw, dw, bs,
    in_ref, proj_ref,
    sx, sg, rx, rg, dfull, bfull, gfull, ufull, pre, act_a, act_b, hid, ggrad, ugrad,
    rs, rr, terms, psend, prec,
    local_sem, dy_s, dy_r, x_s, x_r, down_s, down_r, base_s, base_r,
    gate_s, gate_r, up_s, up_r, ret_s, ret_r, proj_s, proj_r,
):
    my_dp = lax.axis_index("dp")
    me = lax.axis_index("expert")
    rows = n_ex * cp
    tokens, width = tok.shape
    topk = ids.shape[1]
    slots, hidden2 = pre.shape
    hidden = hidden2 // 2
    part = width // n_dp
    nc = part // cw
    rank = bfull.shape[1]
    rk = rank // n_dp
    shift = cp.bit_length() - 1

    def block(owner):
        return pl.ds(pl.multiple_of(owner * cp, cp), cp)

    def wpart(owner):
        return pl.ds(pl.multiple_of(owner * part, part), part)

    def ex_peer(k):
        return lax.rem(me + k, n_ex)

    def ex_from(k):
        return lax.rem(me + n_ex - k, n_ex)

    def dp_peer(i):
        return lax.rem(my_dp + i, n_dp)

    def dp_from(i):
        return lax.rem(my_dp + n_dp - i, n_dp)

    barrier = pltpu.get_barrier_semaphore()

    @pl.loop(1, n_ex)
    def _(k):
        pl.semaphore_signal(barrier, inc=1, device_id={"expert": ex_peer(k)}, device_id_type=MESH)

    for i in range(1, n_dp):
        pl.semaphore_signal(barrier, inc=1, device_id={"dp": dp_peer(i)}, device_id_type=MESH)

    local = [
        pltpu.make_async_copy(pre_h.at[0, 0], pre, local_sem.at[0]),
        pltpu.make_async_copy(dw.at[0], dfull.at[wpart(my_dp)], local_sem.at[1]),
        pltpu.make_async_copy(bs.at[0], bfull.at[wpart(my_dp)], local_sem.at[2]),
    ]
    for c in range(nc):
        src = pl.ds(c * cw, cw)
        local.append(
            pltpu.make_async_copy(gw.at[0, src], gfull.at[my_dp * nc + c], local_sem.at[3 + 2 * c])
        )
        local.append(
            pltpu.make_async_copy(uw.at[0, src], ufull.at[my_dp * nc + c], local_sem.at[4 + 2 * c])
        )
    for copy in local:
        copy.start()

    lane = lax.broadcasted_iota(jnp.int32, (tokens, rows), 1)
    lane_expert = lax.shift_right_logical(lane, shift)
    lane_slot = lax.bitwise_and(lane, cp - 1)
    names = [ids[:, k : k + 1] == lane_expert for k in range(topk)]
    any_name = functools.reduce(jnp.logical_or, names)
    one, zero = jnp.ones((), F32), jnp.zeros((), F32)
    named = jnp.where(any_name, one, zero).astype(BF16)
    below = lax.broadcasted_iota(jnp.int32, (tokens, tokens), 0) > lax.broadcasted_iota(
        jnp.int32, (tokens, tokens), 1
    )
    before = dot(jnp.where(below, one, zero).astype(BF16), named, NN)
    at_slot = before == lane_slot.astype(F32)
    picks = [
        jnp.where(jnp.logical_and(name, at_slot), one, zero).astype(BF16) for name in names
    ]
    pick = jnp.where(jnp.logical_and(any_name, at_slot), one, zero).astype(BF16)
    grads = [
        (og[...].astype(F32) * probs[:, k : k + 1]).astype(BF16) for k in range(topk)
    ]
    sg[...] = dot(jnp.concatenate(picks, axis=0), jnp.concatenate(grads, axis=0), TN).astype(BF16)

    pl.semaphore_wait(barrier, n_ex - 1 + n_dp - 1)

    def down_copy(i, owner, peer):
        return pltpu.make_async_remote_copy(
            dw.at[0], dfull.at[wpart(owner)], down_s.at[i], down_r.at[i],
            device_id={"dp": peer}, device_id_type=MESH,
        )

    def base_copy(i, owner, peer):
        return pltpu.make_async_remote_copy(
            bs.at[0], bfull.at[wpart(owner)], base_s.at[i], base_r.at[i],
            device_id={"dp": peer}, device_id_type=MESH,
        )

    def gate_copy(i, c, owner, peer):
        return pltpu.make_async_remote_copy(
            gw.at[0, pl.ds(c * cw, cw)], gfull.at[owner * nc + c], gate_s.at[i, c], gate_r.at[i, c],
            device_id={"dp": peer}, device_id_type=MESH,
        )

    def up_copy(i, c, owner, peer):
        return pltpu.make_async_remote_copy(
            uw.at[0, pl.ds(c * cw, cw)], ufull.at[owner * nc + c], up_s.at[i, c], up_r.at[i, c],
            device_id={"dp": peer}, device_id_type=MESH,
        )

    def row_copy(src, dst, send, recv, k, peer, owner):
        return pltpu.make_async_remote_copy(
            src.at[block(peer)], dst.at[block(owner)], send.at[k], recv.at[k],
            device_id={"expert": peer}, device_id_type=MESH,
        )

    def ret_copy(n, j, k, peer, owner):
        return pltpu.make_async_remote_copy(
            rs.at[j, block(peer)], rr.at[j, block(owner)], ret_s.at[n, k], ret_r.at[n, k],
            device_id={"expert": peer}, device_id_type=MESH,
        )

    def proj_copy(i, peer):
        return pltpu.make_async_remote_copy(
            psend.at[i], prec.at[i], proj_s.at[i], proj_r.at[i],
            device_id={"dp": peer}, device_id_type=MESH,
        )

    for i in range(1, n_dp):
        down_copy(i, my_dp, dp_peer(i)).start()

    @pl.loop(1, n_ex)
    def _(k):
        row_copy(sg, rg, dy_s, dy_r, k, ex_peer(k), me).start()

    for i in range(1, n_dp):
        base_copy(i, my_dp, dp_peer(i)).start()
    for i in range(1, n_dp):
        for c in range(nc):
            gate_copy(i, c, my_dp, dp_peer(i)).start()
            up_copy(i, c, my_dp, dp_peer(i)).start()

    sx[...] = dot(pick, tok[...], TN).astype(BF16)

    @pl.loop(1, n_ex)
    def _(k):
        row_copy(sx, rx, x_s, x_r, k, ex_peer(k), me).start()

    rg[block(me), :] = sg[block(me), :]
    rx[block(me), :] = sx[block(me), :]

    local[0].wait()
    row = lax.broadcasted_iota(jnp.int32, (rows, slots), 0)
    inner = lax.bitwise_and(row, cp - 1)
    source = lax.shift_right_logical(row, shift) * cap + inner
    spread_mask = jnp.logical_and(
        source == lax.broadcasted_iota(jnp.int32, (rows, slots), 1), inner < cap
    )
    spread = jnp.where(spread_mask, one, zero).astype(BF16)
    fw = 256
    for f in range(0, hidden, fw):
        cols = slice(f, f + fw)
        g = dot(spread, pre[:, f : f + fw], NN)
        u = dot(spread, pre[:, hidden + f : hidden + f + fw], NN)
        sig = jax.nn.sigmoid(g)
        gs = g * sig
        act_a[:, cols] = gs
        hid[:, cols] = (gs * u).astype(BF16)
        act_b[:, cols] = u * sig * (1.0 + g * (1.0 - sig))

    local[1].wait()

    @pl.loop(1, n_ex)
    def _(k):
        row_copy(sg, rg, dy_s, dy_r, k, ex_from(k), ex_from(k)).wait_recv()

    for i in range(1, n_dp):
        down_copy(i, dp_from(i), dp_peer(i)).wait_recv()
    for f in range(0, hidden, fw):
        cols = slice(f, f + fw)
        hg = dot(rg[...], dfull[:, cols], NN)
        ugrad[:, cols] = (hg * act_a[:, cols]).astype(BF16)
        ggrad[:, cols] = (hg * act_b[:, cols]).astype(BF16)

    def row_grad(n, j):
        out = dot(ggrad[...], gfull[j], NT) + dot(ugrad[...], ufull[j], NT)
        rs[j] = out.astype(BF16)

        @pl.loop(1, n_ex)
        def _(k):
            ret_copy(n, j, k, ex_peer(k), me).start()

        rr[j, block(me), :] = rs[j, block(me), :]

    def combine(n, j):
        @pl.loop(1, n_ex)
        def _(k):
            ret_copy(n, j, k, ex_from(k), ex_from(k)).wait_recv()

        cols = pl.ds(pl.multiple_of(j * cw, cw), cw)
        in_ref[:, cols] = dot(pick, rr[j], NN).astype(BF16)

    for c in range(nc):
        local[3 + 2 * c].wait()
        local[4 + 2 * c].wait()
        row_grad(c, my_dp * nc + c)

    local[2].wait()
    for i in range(1, n_dp):
        base_copy(i, dp_from(i), dp_peer(i)).wait_recv()
    dy_proj = dot(rg[...], bfull[...], NN).astype(BF16)
    terms[2] = dot(dy_proj, hid[...], TN)

    @pl.loop(1, n_ex)
    def _(k):
        row_copy(sx, rx, x_s, x_r, k, ex_from(k), ex_from(k)).wait_recv()

    x_proj = dot(rx[...], bfull[...], NN).astype(BF16)
    terms[0] = dot(x_proj, ggrad[...], TN)
    terms[1] = dot(x_proj, ugrad[...], TN)
    for i in range(1, n_dp):
        theirs = pl.ds(pl.multiple_of(dp_peer(i) * rk, rk), rk)
        psend[i] = terms[:, theirs, :].astype(BF16)
        proj_copy(i, dp_peer(i)).start()

    for c in range(nc):
        combine(c, my_dp * nc + c)

    order = [(i, c) for i in range(1, n_dp) for c in range(nc)]
    for n, (i, c) in enumerate(order):
        gate_copy(i, c, dp_from(i), dp_peer(i)).wait_recv()
        up_copy(i, c, dp_from(i), dp_peer(i)).wait_recv()
        row_grad(nc + n, dp_from(i) * nc + c)
        if n:
            last_i, last_c = order[n - 1]
            combine(nc + n - 1, dp_from(last_i) * nc + last_c)
    last_i, last_c = order[-1]
    combine(nc + len(order) - 1, dp_from(last_i) * nc + last_c)

    mine = pl.ds(pl.multiple_of(my_dp * rk, rk), rk)
    total = terms[:, mine, :]
    for i in range(1, n_dp):
        proj_copy(i, dp_peer(i)).wait_recv()
        total = total + prec[i].astype(F32)
    proj_ref[0] = total

    for i in range(1, n_dp):
        down_copy(i, my_dp, dp_peer(i)).wait_send()
        base_copy(i, my_dp, dp_peer(i)).wait_send()
        proj_copy(i, dp_peer(i)).wait_send()
        for c in range(nc):
            gate_copy(i, c, my_dp, dp_peer(i)).wait_send()
            up_copy(i, c, my_dp, dp_peer(i)).wait_send()

    @pl.loop(1, n_ex)
    def _(k):
        row_copy(sg, rg, dy_s, dy_r, k, ex_peer(k), me).wait_send()
        row_copy(sx, rx, x_s, x_r, k, ex_peer(k), me).wait_send()

    spots = [my_dp * nc + c for c in range(nc)] + [dp_from(i) * nc + c for i, c in order]
    for n, j in enumerate(spots):

        @pl.loop(1, n_ex)
        def _(k, n=n, j=j):
            ret_copy(n, j, k, ex_peer(k), me).wait_send()


def body(
    tokens, out_grad, expert_ids, gate_probs, saved_pre, gate_weight, up_weight, down_weight, basis
):
    n_dp, n_ex = lax.axis_size("dp"), lax.axis_size("expert")
    tok_rows, width = tokens.shape
    slots, hidden2 = saved_pre.shape[2:]
    hidden = hidden2 // 2
    cap = slots // n_ex
    cp = max(16, 1 << (cap - 1).bit_length())
    rows = n_ex * cp
    part = gate_weight.shape[1]
    cw = min(256, part)
    nc = part // cw
    chunks = width // cw
    rank = basis.shape[2]
    rk = rank // n_dp
    vmem = pl.BlockSpec(memory_space=pltpu.VMEM)
    hbm = pl.BlockSpec(memory_space=pl.ANY)
    dma = pltpu.SemaphoreType.DMA
    scratch = [
        pltpu.VMEM((rows, width), BF16),
        pltpu.VMEM((rows, width), BF16),
        pltpu.VMEM((rows, width), BF16),
        pltpu.VMEM((rows, width), BF16),
        pltpu.VMEM((width, hidden), BF16),
        pltpu.VMEM((width, rank), BF16),
        pltpu.VMEM((chunks, cw, hidden), BF16),
        pltpu.VMEM((chunks, cw, hidden), BF16),
        pltpu.VMEM((slots, hidden2), BF16),
        pltpu.VMEM((rows, hidden), F32),
        pltpu.VMEM((rows, hidden), F32),
        pltpu.VMEM((rows, hidden), BF16),
        pltpu.VMEM((rows, hidden), BF16),
        pltpu.VMEM((rows, hidden), BF16),
        pltpu.VMEM((chunks, rows, cw), BF16),
        pltpu.VMEM((chunks, rows, cw), BF16),
        pltpu.VMEM((3, rank, hidden), F32),
        pltpu.VMEM((n_dp, 3, rk, hidden), BF16),
        pltpu.VMEM((n_dp, 3, rk, hidden), BF16),
        dma((3 + 2 * nc,)),
        dma((n_ex,)), dma((n_ex,)), dma((n_ex,)), dma((n_ex,)),
        dma((n_dp,)), dma((n_dp,)), dma((n_dp,)), dma((n_dp,)),
        dma((n_dp, nc)), dma((n_dp, nc)), dma((n_dp, nc)), dma((n_dp, nc)),
        dma((chunks, n_ex)), dma((chunks, n_ex)),
        dma((n_dp,)), dma((n_dp,)),
    ]
    return pl.pallas_call(
        functools.partial(kernel, n_dp, n_ex, cap, cp, cw),
        out_shape=(
            jax.ShapeDtypeStruct((tok_rows, width), BF16),
            jax.ShapeDtypeStruct((1, 3, rk, hidden), F32),
        ),
        in_specs=[vmem] * 4 + [hbm] * 5,
        out_specs=(vmem, vmem),
        scratch_shapes=scratch,
        compiler_params=pltpu.CompilerParams(
            collective_id=0, has_side_effects=True, vmem_limit_bytes=60 * 1024 * 1024
        ),
    )(
        expert_ids, gate_probs, tokens, out_grad, saved_pre,
        gate_weight, up_weight, down_weight, basis,
    )


def solution(mesh):
    return jax.shard_map(
        body,
        mesh=mesh,
        in_specs=(
            P(("dp", "expert"), None),
            P(("dp", "expert"), None),
            P(("dp", "expert"), None),
            P(("dp", "expert"), None),
            P("dp", "expert", None, None),
            P("expert", "dp", None),
            P("expert", "dp", None),
            P("expert", "dp", None),
            P("expert", "dp", None),
        ),
        out_specs=(P(("dp", "expert"), None), P("expert", None, "dp", None)),
        check_vma=False,
    )
```

time: 155 us -> 90.2 us (0.58); the launches traced: 153 us -> 89.9 us
  Pallas kernels: 0 us -> 82.4 us
  waiting for transfers between devices: 52.9 us -> 0 us
  starting transfers between devices: 21.5 us -> 0 us
  local copies, waits for them, and re-layouts: 27.4 us -> 6.86 us
  matrix products: 16.3 us -> 0 us
  between operations: 14 us -> 0.64 us
  other arithmetic: 11.4 us -> 0 us
  blocking collectives: 9.46 us -> 0 us
    pallas_call x0 -> x1, Pallas kernels: none -> 82.4 us  [body(): pl.pallas_call(functools.partial(kernel, n_dp, n_ex, cap, cp, cw), out_sh...]
    all_to_all x3 -> x0, waiting for transfers between devices: 50.8 us -> none  [the longest x1 22.6 us: body(): lax.all_to_all(row_grad.astype(jnp.bfloat16).reshape(n_owner, cap, width)...]
    all_to_all x3 -> x0, starting transfers between devices: 21.4 us -> none  [the longest x1 7.4 us: body(): lax.all_to_all(send_rows.reshape(n_owner, cap, width), 'expert', split_ax...]
    dot_general x7 -> x0, matrix products: 16.3 us -> none  [the longest x2 6.64 us: contract_cols(): lax.dot_general(left, right, (((1,), (1,)), ((), ())), preferred_element_...]
    gather x6 -> x0, local copies, waits for them, and re-layouts: 14.2 us -> none  [the longest x1 4.64 us: body(): weight_pick = gate_probs[picked, fill_choice]]
    all_gather x1 -> x0, blocking collectives: 9.46 us -> none  [body(): lax.all_gather(basis, 'dp', axis=1, tiled=True)]
    scatter x2 -> x0, local copies, waits for them, and re-layouts: 5.83 us -> none  [the longest x1 2.91 us: body(): jnp.zeros((n_owner * cap,), jnp.int32).at[target.reshape(-1)]]
    unnamed x16 -> x4, local copies, waits for them, and re-layouts: 1.61 us -> 6.86 us
  transfers between devices with their start and end apart: 7 -> 0, of which waited for: 3 -> 0; matrix products, arithmetic and copies ran while one was open for 35% -> 0% of each run, Pallas kernels for 0% -> 0%
where the time goes in v1:
time: 90.2 us; the launch traced here: 89.9 us
  Pallas kernels  82.4 us (91%)
  local copies, waits for them, and re-layouts  6.86 us (8%)
    pallas_call x1, Pallas kernels, body(): pl.pallas_call(functools.partial(kernel, n_dp, n_ex, cap, cp, cw), out_sh...  82.4 us
    unnamed x4, local copies, waits for them, and re-layouts  6.86 us

profile of v1, /device:TPU:0, one launch (start us, length us, event | category | flops | bytes accessed | tf_op | source)
XLA Modules:
  0.0 89.9 jit_solution(35861401887295335)
XLA Ops:
  0.6 1.4 %copy.11.ids = s32[128,3]{1,0:T(8,128)} copy(s32[128,3]{0,1:T(4,128)} %param.11) | data formatting | bytes 3072 | tf_op args[2]
  2.0 1.4 %copy.12.probs = f32[128,3]{1,0:T(8,128)} copy(f32[128,3]{0,1:T(4,128)} %param.12) | data formatting | bytes 3072 | tf_op args[3]
  3.5 82.4 %shard_map.104 = (bf16[128,1024]{1,0:T(8,128)(2,1)}, f32[1,3,128,768]{3,2,1,0:T(8,128)}) custom-call(s32[128,3]{1,0:T(8,128)} %copy.11.ids, f32[128,3]{1,0:T(8,128)} %copy.12.probs, bf16[128,1024]{1,0:T(8,128)(2,1)} %tok.1, bf16[128,1024]{1,0:T(8,128)(2,1)} %og.1, bf16[1,1,480,1536]{3,2,1,0:T(8,128)(2,1)} %pre_h.1, bf16[1,512,768]{2,1,0:T(8,128)(2,1)} %gw.1, ...), custom_call_target="tpu_custom_call" | custom-call | tf_op jit(solution)/shard_map/pallas_call | solution.py:338
  85.9 1.7 %copy.15 = bf16[128,1024]{1,0:T(8,128)(2,1)} copy(bf16[128,1024]{1,0:T(8,128)(2,1)} %get-tuple-element.4) | data formatting | bytes 524288
  87.6 2.4 %copy.16 = f32[1,3,128,768]{3,2,1,0:T(8,128)} copy(f32[1,3,128,768]{3,2,1,0:T(8,128)} %get-tuple-element.5) | data formatting | bytes 2359296

commit v2 on v1

--- a/solution.py
+++ b/solution.py
@@ -22,10 +22,10 @@
 
 def kernel(
     n_dp, n_ex, cap, cp, cw,
-    ids, probs, tok, og, pre_h, gw, uw, dw, bs,
-    in_ref, proj_ref,
-    sx, sg, rx, rg, dfull, bfull, gfull, ufull, pre, act_a, act_b, hid, ggrad, ugrad,
-    rs, rr, terms, psend, prec,
+    ids, probs, tok_h, og_h, pre_h, gw, uw, dw, bs,
+    in_ref, own_ref, prec,
+    tok, og, sx, sg, rx, rg, dfull, bfull, gfull, ufull, pre, act_a, act_b, hid, ggrad, ugrad,
+    rs, rr, terms, psend,
     local_sem, dy_s, dy_r, x_s, x_r, down_s, down_r, base_s, base_r,
     gate_s, gate_r, up_s, up_r, ret_s, ret_r, proj_s, proj_r,
 ):
@@ -33,7 +33,7 @@
     me = lax.axis_index("expert")
     rows = n_ex * cp
     tokens, width = tok.shape
-    topk = ids.shape[1]
+    topk = ids.shape[0]
     slots, hidden2 = pre.shape
     hidden = hidden2 // 2
     part = width // n_dp
@@ -74,6 +74,13 @@
         pltpu.make_async_copy(dw.at[0], dfull.at[wpart(my_dp)], local_sem.at[1]),
         pltpu.make_async_copy(bs.at[0], bfull.at[wpart(my_dp)], local_sem.at[2]),
     ]
+    local_n = 3 + 2 * nc
+    fetch = [
+        pltpu.make_async_copy(og_h, og, local_sem.at[local_n]),
+        pltpu.make_async_copy(tok_h, tok, local_sem.at[local_n + 1]),
+    ]
+    for copy in fetch:
+        copy.start()
     for c in range(nc):
         src = pl.ds(c * cw, cw)
         local.append(
@@ -85,26 +92,25 @@
     for copy in local:
         copy.start()
 
-    lane = lax.broadcasted_iota(jnp.int32, (tokens, rows), 1)
-    lane_expert = lax.shift_right_logical(lane, shift)
-    lane_slot = lax.bitwise_and(lane, cp - 1)
-    names = [ids[:, k : k + 1] == lane_expert for k in range(topk)]
+    line = lax.broadcasted_iota(jnp.int32, (rows, tokens), 0)
+    line_expert = lax.shift_right_logical(line, shift)
+    line_slot = lax.bitwise_and(line, cp - 1)
+    names = [ids[k : k + 1, :] == line_expert for k in range(topk)]
     any_name = functools.reduce(jnp.logical_or, names)
     one, zero = jnp.ones((), F32), jnp.zeros((), F32)
     named = jnp.where(any_name, one, zero).astype(BF16)
-    below = lax.broadcasted_iota(jnp.int32, (tokens, tokens), 0) > lax.broadcasted_iota(
+    earlier = lax.broadcasted_iota(jnp.int32, (tokens, tokens), 0) < lax.broadcasted_iota(
         jnp.int32, (tokens, tokens), 1
     )
-    before = dot(jnp.where(below, one, zero).astype(BF16), named, NN)
-    at_slot = before == lane_slot.astype(F32)
-    picks = [
-        jnp.where(jnp.logical_and(name, at_slot), one, zero).astype(BF16) for name in names
-    ]
+    before = dot(named, jnp.where(earlier, one, zero).astype(BF16), NN)
+    at_slot = before == line_slot.astype(F32)
     pick = jnp.where(jnp.logical_and(any_name, at_slot), one, zero).astype(BF16)
-    grads = [
-        (og[...].astype(F32) * probs[:, k : k + 1]).astype(BF16) for k in range(topk)
-    ]
-    sg[...] = dot(jnp.concatenate(picks, axis=0), jnp.concatenate(grads, axis=0), TN).astype(BF16)
+    weights = functools.reduce(
+        jnp.add, [jnp.where(name, probs[k : k + 1, :], zero) for k, name in enumerate(names)]
+    )
+    weight = jnp.sum(jnp.where(at_slot, weights, zero), axis=1, keepdims=True)
+    fetch[0].wait()
+    sg[...] = (dot(pick, og[...], NN) * weight).astype(BF16)
 
     pl.semaphore_wait(barrier, n_ex - 1 + n_dp - 1)
 
@@ -146,7 +152,7 @@
 
     def proj_copy(i, peer):
         return pltpu.make_async_remote_copy(
-            psend.at[i], prec.at[i], proj_s.at[i], proj_r.at[i],
+            psend.at[i - 1], prec.at[i - 1], proj_s.at[i], proj_r.at[i],
             device_id={"dp": peer}, device_id_type=MESH,
         )
 
@@ -164,7 +170,8 @@
             gate_copy(i, c, my_dp, dp_peer(i)).start()
             up_copy(i, c, my_dp, dp_peer(i)).start()
 
-    sx[...] = dot(pick, tok[...], TN).astype(BF16)
+    fetch[1].wait()
+    sx[...] = dot(pick, tok[...], NN).astype(BF16)
 
     @pl.loop(1, n_ex)
     def _(k):
@@ -222,7 +229,7 @@
             ret_copy(n, j, k, ex_from(k), ex_from(k)).wait_recv()
 
         cols = pl.ds(pl.multiple_of(j * cw, cw), cw)
-        in_ref[:, cols] = dot(pick, rr[j], NN).astype(BF16)
+        in_ref[:, cols] = dot(pick, rr[j], TN).astype(BF16)
 
     for c in range(nc):
         local[3 + 2 * c].wait()
@@ -244,8 +251,13 @@
     terms[1] = dot(x_proj, ugrad[...], TN)
     for i in range(1, n_dp):
         theirs = pl.ds(pl.multiple_of(dp_peer(i) * rk, rk), rk)
-        psend[i] = terms[:, theirs, :].astype(BF16)
+        psend[i - 1] = terms[:, theirs, :].astype(BF16)
         proj_copy(i, dp_peer(i)).start()
+    mine = pl.ds(pl.multiple_of(my_dp * rk, rk), rk)
+    own_copy = pltpu.make_async_copy(
+        terms.at[:, mine, :], own_ref, local_sem.at[local_n + 2]
+    )
+    own_copy.start()
 
     for c in range(nc):
         combine(c, my_dp * nc + c)
@@ -261,12 +273,9 @@
     last_i, last_c = order[-1]
     combine(nc + len(order) - 1, dp_from(last_i) * nc + last_c)
 
-    mine = pl.ds(pl.multiple_of(my_dp * rk, rk), rk)
-    total = terms[:, mine, :]
+    own_copy.wait()
     for i in range(1, n_dp):
         proj_copy(i, dp_peer(i)).wait_recv()
-        total = total + prec[i].astype(F32)
-    proj_ref[0] = total
 
     for i in range(1, n_dp):
         down_copy(i, my_dp, dp_peer(i)).wait_send()
@@ -287,6 +296,16 @@
         @pl.loop(1, n_ex)
         def _(k, n=n, j=j):
             ret_copy(n, j, k, ex_peer(k), me).wait_send()
+
+
+def finish(n_peers, in_h, own, prec, in_ref, proj_ref, sem):
+    copy = pltpu.make_async_copy(in_h, in_ref, sem)
+    copy.start()
+    total = own[...]
+    for i in range(n_peers):
+        total = total + prec[i].astype(F32)
+    proj_ref[0] = total
+    copy.wait()
 
 
 def body(
@@ -309,6 +328,8 @@
     hbm = pl.BlockSpec(memory_space=pl.ANY)
     dma = pltpu.SemaphoreType.DMA
     scratch = [
+        pltpu.VMEM((tok_rows, width), BF16),
+        pltpu.VMEM((tok_rows, width), BF16),
         pltpu.VMEM((rows, width), BF16),
         pltpu.VMEM((rows, width), BF16),
         pltpu.VMEM((rows, width), BF16),
@@ -326,31 +347,41 @@
         pltpu.VMEM((chunks, rows, cw), BF16),
         pltpu.VMEM((chunks, rows, cw), BF16),
         pltpu.VMEM((3, rank, hidden), F32),
-        pltpu.VMEM((n_dp, 3, rk, hidden), BF16),
-        pltpu.VMEM((n_dp, 3, rk, hidden), BF16),
-        dma((3 + 2 * nc,)),
+        pltpu.VMEM((n_dp - 1, 3, rk, hidden), BF16),
+        dma((6 + 2 * nc,)),
         dma((n_ex,)), dma((n_ex,)), dma((n_ex,)), dma((n_ex,)),
         dma((n_dp,)), dma((n_dp,)), dma((n_dp,)), dma((n_dp,)),
         dma((n_dp, nc)), dma((n_dp, nc)), dma((n_dp, nc)), dma((n_dp, nc)),
         dma((chunks, n_ex)), dma((chunks, n_ex)),
         dma((n_dp,)), dma((n_dp,)),
     ]
-    return pl.pallas_call(
+    in_part, own, received = pl.pallas_call(
         functools.partial(kernel, n_dp, n_ex, cap, cp, cw),
         out_shape=(
             jax.ShapeDtypeStruct((tok_rows, width), BF16),
-            jax.ShapeDtypeStruct((1, 3, rk, hidden), F32),
+            jax.ShapeDtypeStruct((3, rk, hidden), F32),
+            jax.ShapeDtypeStruct((n_dp - 1, 3, rk, hidden), BF16),
         ),
-        in_specs=[vmem] * 4 + [hbm] * 5,
-        out_specs=(vmem, vmem),
+        in_specs=[vmem] * 2 + [hbm] * 7,
+        out_specs=(vmem, hbm, hbm),
         scratch_shapes=scratch,
         compiler_params=pltpu.CompilerParams(
             collective_id=0, has_side_effects=True, vmem_limit_bytes=60 * 1024 * 1024
         ),
     )(
-        expert_ids, gate_probs, tokens, out_grad, saved_pre,
+        expert_ids.T, gate_probs.T, tokens, out_grad, saved_pre,
         gate_weight, up_weight, down_weight, basis,
     )
+    return pl.pallas_call(
+        functools.partial(finish, n_dp - 1),
+        out_shape=(
+            jax.ShapeDtypeStruct((tok_rows, width), BF16),
+            jax.ShapeDtypeStruct((1, 3, rk, hidden), F32),
+        ),
+        in_specs=[hbm, vmem, vmem],
+        out_specs=(vmem, vmem),
+        scratch_shapes=[dma],
+    )(in_part, own, received)
 
 
 def solution(mesh):

time: 90.2 us -> 86 us (0.953)
  local copies, waits for them, and re-layouts: 6.86 us -> 0 us
  Pallas kernels: 82.4 us -> 85.2 us
    unnamed x4 -> x0, local copies, waits for them, and re-layouts: 6.86 us -> none
    pallas_call x0 -> x1, Pallas kernels: none -> 3.48 us  [body(): pl.pallas_call(functools.partial(finish, n_dp - 1), out_shape=(jax.ShapeD...]
where the time goes in v2:
time: 86 us; the launch traced here: 85.8 us
  Pallas kernels  85.2 us (99%)
    pallas_call x1, Pallas kernels, body(): pl.pallas_call(functools.partial(kernel, n_dp, n_ex, cap, cp, cw), out_sh...  81.7 us
    pallas_call x1, Pallas kernels, body(): pl.pallas_call(functools.partial(finish, n_dp - 1), out_shape=(jax.ShapeD...  3.48 us

profile of v2, /device:TPU:0, one launch (start us, length us, event | category | flops | bytes accessed | tf_op | source)
XLA Modules:
  0.0 85.8 jit_solution(14692187626683255501)
XLA Ops:
  0.6 81.7 %shard_map.104 = (bf16[128,1024]{1,0:T(8,128)(2,1)}, f32[3,128,768]{2,1,0:T(8,128)}, bf16[1,3,128,768]{3,2,1,0:T(8,128)(2,1)}) custom-call(s32[3,128]{1,0:T(4,128)} %bitcast.2, f32[3,128]{1,0:T(4,128)} %bitcast.3, bf16[128,1024]{1,0:T(8,128)(2,1)} %tok_h.1, bf16[128,1024]{1,0:T(8,128)(2,1)} %og_h.1, bf16[1,1,480,1536]{3,2,1,0:T(8,128)(2,1)} %pre_h.1, ...), custom_call_target="tpu_custom_call" | custom-call | tf_op jit(solution)/shard_map/pallas_call | solution.py:358
  82.3 3.5 %shard_map.105 = (bf16[128,1024]{1,0:T(8,128)(2,1)}, f32[1,3,128,768]{3,2,1,0:T(8,128)}) custom-call(bf16[128,1024]{1,0:T(8,128)(2,1)} %get-tuple-element.5.in_h, f32[3,128,768]{2,1,0:T(8,128)} %get-tuple-element.6.own, bf16[1,3,128,768]{3,2,1,0:T(8,128)(2,1)} %get-tuple-element.7.prec), custom_call_target="tpu_custom_call" | custom-call | tf_op jit(solution)/shard_map/pallas_call | solution.py:375

commit v3 on v2

--- a/solution.py
+++ b/solution.py
@@ -23,11 +23,11 @@
 def kernel(
     n_dp, n_ex, cap, cp, cw,
     ids, probs, tok_h, og_h, pre_h, gw, uw, dw, bs,
-    in_ref, own_ref, prec,
-    tok, og, sx, sg, rx, rg, dfull, bfull, gfull, ufull, pre, act_a, act_b, hid, ggrad, ugrad,
+    in_h, own_ref, prec,
+    in_v, tok, og, sx, sg, rx, rg, dfull, bfull, gfull, ufull, pre, act_a, act_b, hid, ggrad, ugrad,
     rs, rr, terms, psend,
     local_sem, dy_s, dy_r, x_s, x_r, down_s, down_r, base_s, base_r,
-    gate_s, gate_r, up_s, up_r, ret_s, ret_r, proj_s, proj_r,
+    gate_s, gate_r, up_s, up_r, ret_s, ret_r, proj_s, proj_r, in_s,
 ):
     my_dp = lax.axis_index("dp")
     me = lax.axis_index("expert")
@@ -223,13 +223,17 @@
 
         rr[j, block(me), :] = rs[j, block(me), :]
 
+    stored = []
+
     def combine(n, j):
         @pl.loop(1, n_ex)
         def _(k):
             ret_copy(n, j, k, ex_from(k), ex_from(k)).wait_recv()
 
         cols = pl.ds(pl.multiple_of(j * cw, cw), cw)
-        in_ref[:, cols] = dot(pick, rr[j], TN).astype(BF16)
+        in_v[j] = dot(pick, rr[j], TN).astype(BF16)
+        stored.append(pltpu.make_async_copy(in_v.at[j], in_h.at[:, cols], in_s.at[n]))
+        stored[-1].start()
 
     for c in range(nc):
         local[3 + 2 * c].wait()
@@ -273,14 +277,9 @@
     last_i, last_c = order[-1]
     combine(nc + len(order) - 1, dp_from(last_i) * nc + last_c)
 
-    own_copy.wait()
-    for i in range(1, n_dp):
-        proj_copy(i, dp_peer(i)).wait_recv()
-
     for i in range(1, n_dp):
         down_copy(i, my_dp, dp_peer(i)).wait_send()
         base_copy(i, my_dp, dp_peer(i)).wait_send()
-        proj_copy(i, dp_peer(i)).wait_send()
         for c in range(nc):
             gate_copy(i, c, my_dp, dp_peer(i)).wait_send()
             up_copy(i, c, my_dp, dp_peer(i)).wait_send()
@@ -297,15 +296,42 @@
         def _(k, n=n, j=j):
             ret_copy(n, j, k, ex_peer(k), me).wait_send()
 
-
-def finish(n_peers, in_h, own, prec, in_ref, proj_ref, sem):
-    copy = pltpu.make_async_copy(in_h, in_ref, sem)
-    copy.start()
-    total = own[...]
-    for i in range(n_peers):
-        total = total + prec[i].astype(F32)
-    proj_ref[0] = total
-    copy.wait()
+    for copy in stored:
+        copy.wait()
+    own_copy.wait()
+    for i in range(1, n_dp):
+        proj_copy(i, dp_peer(i)).wait_recv()
+        proj_copy(i, dp_peer(i)).wait_send()
+
+
+def finish(n_peers, in_h, own_h, prec_h, in_ref, proj_ref, rows, own, prec, total, in_s, own_s, prec_s, out_s):
+    loads = []
+    for t in range(own.shape[0]):
+        pieces = [pltpu.make_async_copy(own_h.at[t], own.at[t], own_s.at[t])]
+        for i in range(n_peers):
+            pieces.append(
+                pltpu.make_async_copy(prec_h.at[i, t], prec.at[i, t], prec_s.at[i, t])
+            )
+        for copy in pieces:
+            copy.start()
+        loads.append(pieces)
+    load = pltpu.make_async_copy(in_h, rows, in_s.at[0])
+    load.start()
+    stores = []
+    for t, pieces in enumerate(loads):
+        for copy in pieces:
+            copy.wait()
+        value = own[t]
+        for i in range(n_peers):
+            value = value + prec[i, t].astype(F32)
+        total[t] = value
+        stores.append(pltpu.make_async_copy(total.at[t], proj_ref.at[0, t], out_s.at[t]))
+        stores[-1].start()
+    load.wait()
+    stores.append(pltpu.make_async_copy(rows, in_ref, in_s.at[1]))
+    stores[-1].start()
+    for copy in stores:
+        copy.wait()
 
 
 def body(
@@ -328,6 +354,7 @@
     hbm = pl.BlockSpec(memory_space=pl.ANY)
     dma = pltpu.SemaphoreType.DMA
     scratch = [
+        pltpu.VMEM((chunks, tok_rows, cw), BF16),
         pltpu.VMEM((tok_rows, width), BF16),
         pltpu.VMEM((tok_rows, width), BF16),
         pltpu.VMEM((rows, width), BF16),
@@ -353,7 +380,7 @@
         dma((n_dp,)), dma((n_dp,)), dma((n_dp,)), dma((n_dp,)),
         dma((n_dp, nc)), dma((n_dp, nc)), dma((n_dp, nc)), dma((n_dp, nc)),
         dma((chunks, n_ex)), dma((chunks, n_ex)),
-        dma((n_dp,)), dma((n_dp,)),
+        dma((n_dp,)), dma((n_dp,)), dma((chunks,)),
     ]
     in_part, own, received = pl.pallas_call(
         functools.partial(kernel, n_dp, n_ex, cap, cp, cw),
@@ -363,7 +390,7 @@
             jax.ShapeDtypeStruct((n_dp - 1, 3, rk, hidden), BF16),
         ),
         in_specs=[vmem] * 2 + [hbm] * 7,
-        out_specs=(vmem, hbm, hbm),
+        out_specs=(hbm, hbm, hbm),
         scratch_shapes=scratch,
         compiler_params=pltpu.CompilerParams(
             collective_id=0, has_side_effects=True, vmem_limit_bytes=60 * 1024 * 1024
@@ -378,9 +405,15 @@
             jax.ShapeDtypeStruct((tok_rows, width), BF16),
             jax.ShapeDtypeStruct((1, 3, rk, hidden), F32),
         ),
-        in_specs=[hbm, vmem, vmem],
-        out_specs=(vmem, vmem),
-        scratch_shapes=[dma],
+        in_specs=[hbm, hbm, hbm],
+        out_specs=(hbm, hbm),
+        scratch_shapes=[
+            pltpu.VMEM((tok_rows, width), BF16),
+            pltpu.VMEM((3, rk, hidden), F32),
+            pltpu.VMEM((n_dp - 1, 3, rk, hidden), BF16),
+            pltpu.VMEM((3, rk, hidden), F32),
+            dma((2,)), dma((3,)), dma((n_dp - 1, 3)), dma((3,)),
+        ],
     )(in_part, own, received)
 
 

time: 86 us -> 83.7 us (0.973)
  Pallas kernels: 85.2 us -> 82.8 us
    pallas_call x1, Pallas kernels: 81.7 us -> 80.4 us  [body(): pl.pallas_call(functools.partial(kernel, n_dp, n_ex, cap, cp, cw), out_sh...]
    pallas_call x1, Pallas kernels: 3.48 us -> 2.4 us  [body(): pl.pallas_call(functools.partial(finish, n_dp - 1), out_shape=(jax.ShapeD...]
where the time goes in v3:
time: 83.7 us; the launch traced here: 83.5 us
  Pallas kernels  82.8 us (99%)
    pallas_call x1, Pallas kernels, body(): pl.pallas_call(functools.partial(kernel, n_dp, n_ex, cap, cp, cw), out_sh...  80.4 us
    pallas_call x1, Pallas kernels, body(): pl.pallas_call(functools.partial(finish, n_dp - 1), out_shape=(jax.ShapeD...  2.4 us

profile of v3, /device:TPU:0, one launch (start us, length us, event | category | flops | bytes accessed | tf_op | source)
XLA Modules:
  0.0 83.5 jit_solution(4506082969903162525)
XLA Ops:
  0.6 80.4 %shard_map.104 = (bf16[128,1024]{1,0:T(8,128)(2,1)}, f32[3,128,768]{2,1,0:T(8,128)}, bf16[1,3,128,768]{3,2,1,0:T(8,128)(2,1)}) custom-call(s32[3,128]{1,0:T(4,128)} %bitcast.2, f32[3,128]{1,0:T(4,128)} %bitcast.3, bf16[128,1024]{1,0:T(8,128)(2,1)} %tok_h.1, bf16[128,1024]{1,0:T(8,128)(2,1)} %og_h.1, bf16[1,1,480,1536]{3,2,1,0:T(8,128)(2,1)} %pre_h.1, ...), custom_call_target="tpu_custom_call" | custom-call | tf_op jit(solution)/shard_map/pallas_call | solution.py:385
  81.1 2.4 %shard_map.105 = (bf16[128,1024]{1,0:T(8,128)(2,1)}, f32[1,3,128,768]{3,2,1,0:T(8,128)}) custom-call(bf16[128,1024]{1,0:T(8,128)(2,1)} %get-tuple-element.5.in_h, f32[3,128,768]{2,1,0:T(8,128)} %get-tuple-element.6.own_h, bf16[1,3,128,768]{3,2,1,0:T(8,128)(2,1)} %get-tuple-element.7.prec_h), custom_call_target="tpu_custom_call" | custom-call | tf_op jit(solution)/shard_map/pallas_call | solution.py:402
